TPU v7x, 32 devices: a whole 2x2x4 slice. The times are simulated.
32 devices in a mesh: dp: 2 (over x), expert: 16 (over z, y, core).
Axes of the slice: x: 2, y: 2, z: 4, core: 2. Of those that a mesh axis runs over, the one named last changes fastest.
Arguments:
- hidden: bfloat16 [2, 1024, 2, 2048], P('dp', 'expert'), may hold values from -6 to 6
- queries: bfloat16 [2, 1024, 2, 4096], P('dp', 'expert'), may hold values from -45 to 45
- latents: bfloat16 [2, 1024, 2, 512], P('dp', 'expert'), may hold values from -165 to 165
- mem_latents: bfloat16 [2, 32, 2, 512], P('dp'), may hold values from -6 to 6
- lengths: int32 [2, 2], P('dp'), may hold values from 512 to 1024
- ids: int32 [2, 1024, 2, 6], P('dp', 'expert'), may hold values from 0 to 15, all different within a row; in each aligned block of 128 rows (0 to 127, 128 to 255, ..., all dimensions but the last counted through in order) at most 50 rows name the same one
- gates: bfloat16 [2, 1024, 2, 6], P('dp', 'expert'), may hold values from 0.049804688 to 0.5
- norm_gain: bfloat16 [2048], replicated, may hold values from 0.25 to 1.75
- w_uv: bfloat16 [8, 512, 128], P('dp'), may hold values from -0.25 to 0.25
- w_out: bfloat16 [1024, 2048], P('dp'), may hold values from -0.1875 to 0.1875
- w_gate: bfloat16 [16, 2048, 704], P('expert'), may hold values from -0.125 to 0.125
- w_up: bfloat16 [16, 2048, 704], P('expert'), may hold values from -0.125 to 0.125
- w_down: bfloat16 [16, 704, 2048], P('expert'), may hold values from -0.21875 to 0.21875
Outputs:
- layer_out: bfloat16 [2, 1024, 2, 2048], P('dp', 'expert')
Inputs may be any that keep to these rules, and one draw needn't show every extreme that they name: `ids`: each row names 6 different experts; the rows of one device (aligned blocks of 128 rows in the order of the leading dimensions) name any one expert at most 50 times, a bound that some block reaches.
All inputs are finite; a program needn't handle non-finite values.
Results may differ from a plain program's by a relative error of at most 0.007.
Values may be sent and summed in bfloat16 or wider, within the bound.
A program may use at most 128 MiB of HBM per device.

v0:
```python
import jax
import jax.numpy as jnp
from jax import lax
from jax.sharding import PartitionSpec as P

score_scale = 192.0 ** (-0.5)
norm_eps = 1e-06


def shards(
    hidden,
    queries,
    latents,
    mem_latents,
    lengths,
    ids,
    gates,
    norm_gain,
    w_uv,
    w_out,
    w_gate,
    w_up,
    w_down,
):
    local_len = hidden.shape[1]
    seq_count = hidden.shape[2]
    model_width = hidden.shape[3]
    latent_dim = latents.shape[3]
    head_count = queries.shape[3] // latent_dim
    row_count = local_len * seq_count
    owner_count = lax.axis_size("expert")
    shard_index = lax.axis_index("expert")
    own_pos = shard_index * local_len + jnp.arange(local_len, dtype=jnp.int32)
    query_rows = queries[0].reshape(local_len, seq_count, head_count, latent_dim)
    memory = mem_latents[0]
    seq_limit = lengths[0]
    mem_scores = (
        jnp.einsum("tshl,msl->shtm", query_rows, memory, preferred_element_type=jnp.float32)
        * score_scale
    )
    first_max = jnp.max(mem_scores, axis=3)
    mem_weights = jnp.exp(mem_scores - first_max[..., None])
    first_sum = jnp.sum(mem_weights, axis=3)
    first_acc = jnp.einsum(
        "shtm,msl->tshl",
        mem_weights.astype(jnp.bfloat16),
        memory,
        preferred_element_type=jnp.float32,
    )

    def fold_step(carry, portion):
        old_max, old_sum, old_acc = carry
        key_rows = portion[0]
        key_pos = jnp.arange(key_rows.shape[0], dtype=jnp.int32)
        scores = (
            jnp.einsum("tshl,jsl->shtj", query_rows, key_rows, preferred_element_type=jnp.float32)
            * score_scale
        )
        causal = key_pos[None, :] <= own_pos[:, None]
        inside = key_pos[None, :] < seq_limit[:, None]
        visible = causal[None, None, :, :] & inside[:, None, None, :]
        scores = jnp.where(visible, scores, -jnp.inf)
        new_max = jnp.maximum(old_max, jnp.max(scores, axis=3))
        weights = jnp.exp(scores - new_max[..., None])
        factor = jnp.exp(old_max - new_max)
        new_sum = old_sum * factor + jnp.sum(weights, axis=3)
        contrib = jnp.einsum(
            "shtj,jsl->tshl",
            weights.astype(jnp.bfloat16),
            key_rows,
            preferred_element_type=jnp.float32,
        )
        new_acc = old_acc * jnp.transpose(factor, (2, 0, 1))[..., None] + contrib
        return (new_max, new_sum, new_acc)

    portion = lax.all_gather(latents, "expert", axis=1, tiled=True)
    last_pos = jnp.max(own_pos)
    final_max, final_sum, final_acc = lax.cond(
        jnp.int32(0) <= last_pos,
        lambda state: fold_step(state, portion),
        lambda state: state,
        (first_max, first_sum, first_acc),
    )
    attended = (final_acc / jnp.transpose(final_sum, (2, 0, 1))[..., None]).astype(jnp.bfloat16)
    moved_heads = lax.all_to_all(attended, "dp", split_axis=2, concat_axis=0, tiled=True)
    local_values = jnp.einsum(
        "tshl,hlv->tshv", moved_heads, w_uv, preferred_element_type=jnp.float32
    ).astype(jnp.bfloat16)
    flat_local = local_values.reshape(moved_heads.shape[0] * seq_count, -1)
    attn_out = lax.psum_scatter(
        jnp.dot(flat_local, w_out, preferred_element_type=jnp.float32).astype(jnp.bfloat16),
        "dp",
        scatter_dimension=0,
        tiled=True,
    ).astype(jnp.float32)
    residual = hidden[0].reshape(row_count, model_width).astype(jnp.float32) + attn_out
    mean_square = jnp.mean(residual * residual, axis=-1, keepdims=True)
    normed = (residual * lax.rsqrt(mean_square + norm_eps) * norm_gain.astype(jnp.float32)).astype(
        jnp.bfloat16
    )
    experts_here = w_gate.shape[0]
    expert_count = owner_count * experts_here
    top_count = ids.shape[3]
    capacity = min(row_count, row_count * top_count // expert_count + 2)
    flat_ids = ids[0].reshape(row_count * top_count)
    onehot = (flat_ids[:, None] == jnp.arange(expert_count, dtype=jnp.int32)[None, :]).astype(
        jnp.int32
    )
    before = jnp.cumsum(onehot, axis=0) - onehot
    slot_within = jnp.sum(before * onehot, axis=1)
    slot_index = (flat_ids * capacity + slot_within).reshape(row_count, top_count)
    matching = (
        jnp.arange(expert_count * capacity, dtype=jnp.int32)[:, None, None]
        == slot_index[None, :, :]
    )
    placing = jnp.any(matching, axis=2).astype(jnp.bfloat16)
    gate_rows = gates[0].reshape(row_count, top_count).astype(jnp.float32)
    mixing = jnp.sum(jnp.where(matching, gate_rows[None, :, :], jnp.float32(0.0)), axis=2).astype(
        jnp.bfloat16
    )
    outgoing = jnp.dot(placing, normed, preferred_element_type=jnp.float32).astype(jnp.bfloat16)
    outgoing = outgoing.reshape(owner_count, experts_here, capacity, model_width)
    incoming = lax.all_to_all(outgoing, "expert", split_axis=0, concat_axis=0, tiled=True)
    gate_h = jnp.einsum("necd,edf->necf", incoming, w_gate, preferred_element_type=jnp.float32)
    up_h = jnp.einsum("necd,edf->necf", incoming, w_up, preferred_element_type=jnp.float32)
    act = (jax.nn.silu(gate_h) * up_h).astype(jnp.bfloat16)
    produced = jnp.einsum("necf,efd->necd", act, w_down, preferred_element_type=jnp.float32).astype(
        jnp.bfloat16
    )
    returned = lax.all_to_all(produced, "expert", split_axis=0, concat_axis=0, tiled=True)
    combined_rows = returned.reshape(expert_count * capacity, model_width)
    routed = jnp.einsum("st,sd->td", mixing, combined_rows, preferred_element_type=jnp.float32)
    layer_out = (residual + routed).astype(jnp.bfloat16)
    return layer_out.reshape(1, local_len, seq_count, model_width)


def solution(mesh):
    return jax.shard_map(
        shards,
        mesh=mesh,
        in_specs=(
            P("dp", "expert", None, None),
            P("dp", "expert", None, None),
            P("dp", "expert", None, None),
            P("dp", None, None, None),
            P("dp", None),
            P("dp", "expert", None, None),
            P("dp", "expert", None, None),
            P(),
            P("dp", None, None),
            P("dp", None),
            P("expert", None, None),
            P("expert", None, None),
            P("expert", None, None),
        ),
        out_specs=P("dp", "expert", None, None),
        check_vma=False,
    )
```

profile of v0, /device:TPU:13, one launch (start us, length us, event | category | flops | bytes accessed | tf_op | source)
XLA Modules:
  0.0 317.8 jit_solution(8418146829069488297)
XLA Ops:
  6.5 1.7 copy.53
  8.4 2.6 reshape.146
  11.0 0.6 fusion.66
  12.2 2.5 fusion.67
  14.8 0.1 fusion.55
  14.9 1.8 convolution_bitcast_fusion
  16.7 34.0 %all-gather.2.cloned.1.call-done = bf16[1,1024,2,512]{3,1,2,0:T(8,128)(2,1)} async-done(((bf16[1,64,2,512]{3,1,2,0:T(8,128)(2,1)}), bf16[1,1024,2,512]{3,1,2,0:T(8,128)(2,1)}) %all-gather.2.cloned.1.call-update) | async-done | bytes 2097168 | tf_op jit(solution)/shard_map/all_gather | solution.py:76
  50.6 8.0 %conditional.1 = (f32[2,8,64]{2,1,0:T(8,128)S(1)}, f32[64,2,8,512]{3,0,1,2:T(8,128)S(1)}) conditional(s32[]{:T(128)} %convert_element_type.80, (f32[2,8,64]{2,1,0:T(8,128)S(1)}, f32[64,2,8,512]{3,0,2,1:T(8,128)}) %tuple.12, (s32[64]{0:T(128)S(1)}, s32[1,2]{1,0:T(1,128)S(1)}, bf16[1,1024,2,512]{3,1,2,0:T(8,128)(2,1)}, ...), branch_computations={%region_3.0_spmd, %region_4.7_spmd} | conditional | flops 2160268288 | bytes 43708752 | solution.py:78
  50.6 0.1 iota_compare_fusion
  50.7 0.1 iota_compare_fusion.1
  50.8 0.1 broadcast_and_fusion
  50.9 3.7 %fusion.2 = (f32[2,8,64]{2,1,0:T(8,128)S(1)}, f32[2,1024,64,8]{1,2,3,0:T(8,128)S(1)}) fusion(pred[2,64,1024]{2,1,0:T(8,128)(4,1)S(1)} %broadcast_and_fusion, bf16[64,2,8,512]{3,2,1,0:T(8,128)(2,1)} %get-tuple-element.60, bf16[1,1024,2,512]{3,1,2,0:T(8,128)(2,1)} %get-tuple-element.27), kind=kOutput, calls=%fused_computation.4 | convolution fusion | flops 1076886528 | bytes 7475200 | tf_op jit(solution)/shard_map/cond/branch_1_fun/tshl,jsl->shtj/dot_general | solution.py:56
  54.6 1.1 fusion.1
  55.7 0.5 copy-done.1
  56.2 0.6 copy-done.13
  56.8 1.6 bitcast_add_fusion
  58.4 0.2 copy.79
  58.6 0.2 divide_convert_fusion
  58.9 16.0 %all_to_all.28 = bf16[64,2,8,512]{3,0,1,2:T(8,128)(2,1)S(1)} all-to-all(bf16[64,2,8,512]{3,0,1,2:T(8,128)(2,1)S(1)} %divide_convert_fusion), channel_id=1, replica_groups=mesh['dp'=2,'expert'=16] {'dp'}, dimensions={2} | all-to-all | bytes 2097152 | tf_op jit(solution)/shard_map/all_to_all | solution.py:85
  74.9 0.1 copy.57
  75.0 0.4 fusion.42
  75.4 0.2 copy.58
  75.7 1.7 convolution_convert_fusion.1
  77.4 0.1 copy.60
  77.5 0.1 eq.43
  77.7 0.1 eq.39
  77.8 1.1 reshape.137
  79.0 1.7 reduce-window.6
  80.7 0.3 slice_reduce_fusion
  81.0 0.1 fusion.63
  81.1 0.1 reduce_sum.49
  81.2 0.1 copy.59
  81.4 0.4 fusion.31
  81.9 16.1 %reduce-scatter.2.cloned.1.call-done = bf16[128,2048]{1,0:T(8,128)(2,1)} async-done(((bf16[256,2048]{1,0:T(8,128)(2,1)}), bf16[128,2048]{1,0:T(8,128)(2,1)}) %reduce-scatter.2.cloned.1.call-update) | async-done | bytes 524304 | tf_op jit(solution)/shard_map/reduce_scatter | solution.py:90
  98.0 1.6 multiply_reduce_fusion
  99.6 4.2 %convolution_convert_fusion = bf16[800,2048]{1,0:T(8,128)(2,1)} fusion(pred[800,128]{1,0:T(8,128)(4,1)S(1)} %fusion.31, f32[2048]{0:T(1024)S(1)} %convert_element_type.92, f32[128]{0:T(128)S(1)} %add_rsqrt_fusion, f32[128,2048]{1,0:T(8,128)} %reshape.137, bf16[128,2048]{1,0:T(8,128)(2,1)} %reduce-scatter.2.cloned.1.call-done), kind=kOutput, calls=%fused_computation.28 | convolution fusion | flops 422379520 | bytes 4960768 | tf_op jit(solution)/shard_map/dot_general | solution.py:121
  103.8 4.7 %reshape.129 = bf16[16,1,50,2048]{3,2,0,1:T(8,128)(2,1)} reshape(bf16[800,2048]{1,0:T(8,128)(2,1)} %convolution_convert_fusion) | data formatting | bytes 6553600 | tf_op jit(solution)/shard_map/reshape | solution.py:122
  108.5 87.7 %all_to_all.29 = bf16[16,1,50,2048]{3,2,1,0:T(8,128)(2,1)S(1)} all-to-all(bf16[16,1,50,2048]{3,2,1,0:T(8,128)(2,1)} %bitcast.155), channel_id=1, replica_groups=mesh['dp'=2,'expert'=16] {'expert'}, dimensions={0} | all-to-all | bytes 6553600 | tf_op jit(solution)/shard_map/all_to_all | solution.py:123
  196.2 1.8 copy-done.3
  198.0 4.6 %fusion.22 = f32[16,50,704]{2,1,0:T(8,128)} fusion(bf16[16,1,50,2048]{3,2,1,0:T(8,128)(2,1)S(1)} %all_to_all.29, bf16[1,2048,704]{1,2,0:T(8,128)(2,1)S(1)} %copy-done.12), kind=kOutput, calls=%fused_computation.25 | convolution fusion | flops 2306867200 | bytes 8413184 | tf_op jit(solution)/shard_map/necd,edf->necf/dot_general | solution.py:124
  202.7 11.1 %convert_bitcast_fusion = bf16[16,1,50,2048]{3,2,1,0:T(8,128)(2,1)} fusion(bf16[1,704,2048]{2,1,0:T(8,128)(2,1)S(1)} %copy-done, bf16[1,2048,704]{1,2,0:T(8,128)(2,1)} %param.26, bf16[16,1,50,2048]{3,2,1,0:T(8,128)(2,1)} %copy-done.3, f32[16,50,704]{2,1,0:T(8,128)} %fusion.22), kind=kOutput, calls=%fused_computation.27 | convolution fusion | flops 4618752000 | bytes 14573568 | tf_op jit(solution)/shard_map/necf,efd->necd/dot_general | solution.py:127
  213.8 5.3 %all-to-all-start.2 = ((bf16[16,1,50,2048]{3,2,1,0:T(8,128)(2,1)}), bf16[16,1,50,2048]{3,2,1,0:T(8,128)(2,1)}, u32[]{:S(2)}, u32[]{:S(2)}) async-start(bf16[16,1,50,2048]{3,2,1,0:T(8,128)(2,1)} %convert_bitcast_fusion), calls=%async_computation.3 | async-start | bytes 7340032 | tf_op jit(solution)/shard_map/all_to_all | solution.py:130
  219.1 0.1 copy.64
  219.3 1.0 select_reduce_fusion
  220.3 80.1 %all-to-all-done.2 = bf16[16,1,50,2048]{3,2,1,0:T(8,128)(2,1)} async-done(((bf16[16,1,50,2048]{3,2,1,0:T(8,128)(2,1)}), bf16[16,1,50,2048]{3,2,1,0:T(8,128)(2,1)}, u32[]{:S(2)}, u32[]{:S(2)}) %all-to-all-start.2) | async-done | bytes 3276832 | tf_op jit(solution)/shard_map/all_to_all | solution.py:130
  300.3 4.7 %reshape.135 = bf16[800,2048]{1,0:T(8,128)(2,1)} reshape(bf16[16,1,50,2048]{3,2,1,0:T(8,128)(2,1)} %all-to-all-done.2) | data formatting | bytes 6553600 | tf_op jit(solution)/shard_map/reshape | solution.py:131
  305.0 3.8 %fusion.32 = bf16[128,2048]{1,0:T(8,128)(2,1)} fusion(bf16[800,2048]{1,0:T(8,128)(2,1)} %reshape.135, f32[128,2048]{1,0:T(8,128)} %reshape.137, bf16[128,2048]{1,0:T(8,128)(2,1)S(1)} %copy-done.2, bf16[800,128]{1,0:T(8,128)(2,1)} %select_reduce_fusion), kind=kOutput, calls=%fused_computation.44 | convolution fusion | flops 420478976 | bytes 5578752 | tf_op jit(solution)/shard_map/st,sd->td/dot_general | solution.py:132
  308.8 2.2 reshape.136
  (41 shorter events, 0.3 us)
Async XLA Ops:
  6.5 196.1 %copy-start = (bf16[1,704,2048]{2,1,0:T(8,128)(2,1)S(1)}, bf16[1,704,2048]{2,1,0:T(8,128)(2,1)}, u32[]{:S(2)}) copy-start(bf16[1,704,2048]{2,1,0:T(8,128)(2,1)} %param.27) | copy-start | bytes 8650756
  6.5 8.3 %copy-start.7 = (bf16[1,32,2,512]{3,2,1,0:T(2,128)(2,1)S(1)}, bf16[1,32,2,512]{3,2,1,0:T(2,128)(2,1)}, u32[]{:S(2)}) copy-start(bf16[1,32,2,512]{3,2,1,0:T(2,128)(2,1)} %param.18) | copy-start | bytes 196612
  6.5 44.1 %all-gather.2.cloned.1.call-start = ((), (), s32[]{:S(2)}) async-start(), calls=%async_computation.4 | async-start | bytes 2228224 | tf_op jit(solution)/shard_map/all_gather | solution.py:76
  8.3 89.7 %reduce-scatter.2.cloned.1.call-start = ((), (), s32[]{:S(2)}) async-start(), calls=%async_computation.5 | async-start | bytes 1572864 | tf_op jit(solution)/shard_map/reduce_scatter | solution.py:90
  8.4 42.3 %copy-start.11 = (s32[1,2]{1,0:T(1,128)S(1)}, s32[1,2]{1,0:T(1,128)}, u32[]{:S(2)}) copy-start(s32[1,2]{1,0:T(1,128)} %param.19) | copy-start | bytes 28
  54.6 1.6 copy-start.1
  54.6 2.2 copy-start.13
  58.8 16.1 %copy-start.5 = (bf16[4,512,128]{2,1,0:T(8,128)(2,1)S(1)}, bf16[4,512,128]{2,1,0:T(8,128)(2,1)}, u32[]{:S(2)}) copy-start(bf16[4,512,128]{2,1,0:T(8,128)(2,1)} %param.23) | copy-start | bytes 1572868
  58.9 16.8 %copy-start.4 = (bf16[512,2048]{1,0:T(8,128)(2,1)S(1)}, bf16[512,2048]{1,0:T(8,128)(2,1)}, u32[]{:S(2)}) copy-start(bf16[512,2048]{1,0:T(8,128)(2,1)} %param.24) | copy-start | bytes 6291460
  75.4 2.0 copy-start.8
  75.4 2.4 copy-start.6
  75.7 5.8 %copy-start.9 = (bf16[2048]{0:T(1024)(128)(2,1)S(1)}, bf16[2048]{0:T(1024)(128)(2,1)}, u32[]{:S(2)}) copy-start(bf16[2048]{0:T(1024)(128)(2,1)} %param.22) | copy-start | bytes 12292
  108.5 89.6 %copy-start.12 = (bf16[1,2048,704]{1,2,0:T(8,128)(2,1)S(1)}, bf16[1,2048,704]{1,2,0:T(8,128)(2,1)}, u32[]{:S(2)}) copy-start(bf16[1,2048,704]{1,2,0:T(8,128)(2,1)} %param.25) | copy-start | bytes 8650756
  196.2 1.8 copy-start.3
  213.8 5.3 %copy-start.10 = (bf16[1,64,2,6]{1,2,3,0:T(2,128)(2,1)S(1)}, bf16[1,64,2,6]{1,2,3,0:T(2,128)(2,1)}, u32[]{:S(2)}) copy-start(bf16[1,64,2,6]{1,2,3,0:T(2,128)(2,1)} %param.21) | copy-start | bytes 4612
  213.8 86.5 %all-to-all-start.2 = ((bf16[16,1,50,2048]{3,2,1,0:T(8,128)(2,1)}), bf16[16,1,50,2048]{3,2,1,0:T(8,128)(2,1)}, u32[]{:S(2)}, u32[]{:S(2)}) async-start(bf16[16,1,50,2048]{3,2,1,0:T(8,128)(2,1)} %convert_bitcast_fusion), calls=%async_computation.3 | async-start | bytes 7340032 | tf_op jit(solution)/shard_map/all_to_all | solution.py:130
  220.3 84.7 %copy-start.2 = (bf16[128,2048]{1,0:T(8,128)(2,1)S(1)}, bf16[128,2048]{1,0:T(8,128)(2,1)}, u32[]{:S(2)}) copy-start(bf16[128,2048]{1,0:T(8,128)(2,1)} %reduce-scatter.2.cloned.1.call-done) | copy-start | bytes 1572868
Sparse Core Ops, SparseCore 0:
  9.5 41.0 all-gather.1
  77.5 20.4 reduce-scatter.1
where the time goes:
time: 318 us
  waiting for transfers between devices  130 us (41%)
  blocking collectives  104 us (33%)
  matrix products  35.5 us (11%)
  local copies, waits for them, and re-layouts  21.6 us (7%)
  between operations  14.3 us (4%)
  other arithmetic  7.11 us (2%)
  starting transfers between devices  5.32 us (2%)
    all_to_all x1, blocking collectives, shards(): lax.all_to_all(outgoing, 'expert', split_axis=0, concat_axis=0, tiled=True)  87.7 us
    all_to_all x1, waiting for transfers between devices, shards(): lax.all_to_all(produced, 'expert', split_axis=0, concat_axis=0, tiled=True)  80.1 us
    all_gather x1, waiting for transfers between devices, shards(): portion = lax.all_gather(latents, 'expert', axis=1, tiled=True)  34 us
    reduce_scatter x1, waiting for transfers between devices, shards(): lax.psum_scatter(jnp.dot(flat_local, w_out, preferred_element_type=jnp.fl...  16.1 us
    all_to_all x1, blocking collectives, shards(): lax.all_to_all(attended, 'dp', split_axis=2, concat_axis=0, tiled=True)  16 us
    dot_general x1, matrix products, shards(): jnp.einsum('necf,efd->necd', act, w_down, preferred_element_type=jnp.floa...  11.1 us
  transfers between devices with their start and end apart: 3, of which 3 were waited for; matrix products, arithmetic and copies ran while one was open for 4% of the time, Pallas kernels for 0%

commit v1 on v0

v1 whole, which is shorter than its diff:
```python
import functools

import jax
import jax.numpy as jnp
from jax import lax
from jax.experimental import pallas as pl
from jax.experimental.pallas import tpu as pltpu
from jax.sharding import PartitionSpec as P

score_scale = 192.0 ** (-0.5)
norm_eps = 1e-06
MESH = pl.DeviceIdType.MESH


def ring_place(n):
    chips = n // 2
    depth = chips // 2
    me = lax.axis_index("expert")
    core = me % 2
    chip = me // 2
    row, col = chip // 2, chip % 2
    pos = col * row + (1 - col) * (chips - 1 - row)

    def device(offset, core_of):
        p = (pos + offset + chips) % chips
        q = p // depth
        r = (1 - q) * p + q * (chips - 1 - p)
        return (2 * r + 1 - q) * 2 + core_of

    return me, core, device


def greet(targets):
    barrier = pltpu.get_barrier_semaphore()
    for target in targets:
        pl.semaphore_signal(barrier, inc=1, device_id={"expert": target}, device_id_type=MESH)
    pl.semaphore_wait(barrier, len(targets))


def remote(src, dst, send_sem, recv_sem, target):
    return pltpu.make_async_remote_copy(
        src_ref=src,
        dst_ref=dst,
        send_sem=send_sem,
        recv_sem=recv_sem,
        device_id={"expert": target},
        device_id_type=MESH,
    )


def gather_kernel(n, cut, x_ref, out_ref, ring_send, ring_recv, pair_send, pair_recv, own_sem):
    chips = n // 2
    half_ring = chips // 2
    rows = x_ref.shape[0]
    last = chips - 2
    me, core, device = ring_place(n)
    partner = device(0, 1 - core)
    ahead = (device(1, core), device(-1, core))
    spans = (pl.ds(0, cut), pl.ds(cut, rows - cut))
    greet((ahead[0], ahead[1], partner))

    def arrival(way, j):
        dist, half = (half_ring, way) if j == last else (j // 2 + 1, j % 2)
        return device(-dist if way == 0 else dist, core), spans[half]

    waits = []
    for way in (0, 1):
        for j in (0, 1):
            if j > last:
                continue
            if j == last and half_ring == 1:
                span = spans[way]
            else:
                span = spans[j]
            copy = remote(
                x_ref.at[span], out_ref.at[me, span],
                ring_send.at[way, j], ring_recv.at[way, j], ahead[way],
            )
            copy.start()
            waits.append(copy)
    share = remote(x_ref, out_ref.at[me], pair_send.at[2 * last + 2], pair_recv.at[2 * last + 2], partner)
    share.start()
    waits.append(share)
    keep = pltpu.make_async_copy(x_ref, out_ref.at[me], own_sem)
    keep.start()

    for j in range(last + 1):
        for way in (0, 1):
            slot, span = arrival(way, j)
            piece = out_ref.at[slot, span]
            remote(piece, piece, ring_send.at[way, j], ring_recv.at[way, j], ahead[way]).wait_recv()
            onward = j + 2
            if j >= last - 2 and j < last:
                onward = last if j == last - 2 + way else None
            if j == last:
                onward = None
            if onward is not None:
                copy = remote(piece, piece, ring_send.at[way, onward], ring_recv.at[way, onward], ahead[way])
                copy.start()
                waits.append(copy)
            index = 2 * j + way
            copy = remote(piece, piece, pair_send.at[index], pair_recv.at[index], partner)
            copy.start()
            waits.append(copy)

    for j in range(last + 1):
        for way in (0, 1):
            dist, half = (half_ring, way) if j == last else (j // 2 + 1, j % 2)
            slot = device(-dist if way == 0 else dist, 1 - core)
            piece = out_ref.at[slot, spans[half]]
            index = 2 * j + way
            remote(piece, piece, pair_send.at[index], pair_recv.at[index], partner).wait_recv()
    other = out_ref.at[partner]
    remote(other, other, pair_send.at[2 * last + 2], pair_recv.at[2 * last + 2], partner).wait_recv()
    for copy in waits:
        copy.wait_send()
    keep.wait()


def ring_gather(x, n, cut, collective_id):
    rows, cols = x.shape
    steps = n // 2 - 1
    return pl.pallas_call(
        functools.partial(gather_kernel, n, cut),
        out_shape=jax.ShapeDtypeStruct((n, rows, cols), x.dtype),
        in_specs=[pl.BlockSpec(memory_space=pltpu.VMEM)],
        out_specs=pl.BlockSpec(memory_space=pl.ANY),
        scratch_shapes=[
            pltpu.SemaphoreType.DMA((2, steps)),
            pltpu.SemaphoreType.DMA((2, steps)),
            pltpu.SemaphoreType.DMA((2 * steps + 1,)),
            pltpu.SemaphoreType.DMA((2 * steps + 1,)),
            pltpu.SemaphoreType.DMA,
        ],
        compiler_params=pltpu.CompilerParams(collective_id=collective_id, has_side_effects=True),
        cost_estimate=pl.CostEstimate(flops=0, bytes_accessed=16 * n * rows * cols, transcendentals=0),
        name="ring_gather_%d" % collective_id,
    )(x)


def reduce_kernel(
    n, part_ref, out_ref, mine, paired, arrived, ring_send, ring_recv, pair_send, pair_recv, load_sem
):
    chips = n // 2
    half_ring = chips // 2
    half = mine.shape[1] // 2
    last = chips - 2
    me, core, device = ring_place(n)
    partner = device(0, 1 - core)
    ahead = (device(1, core), device(-1, core))
    greet((ahead[0], ahead[1], partner))

    order = [half_ring]
    for k in range(half_ring - 1, 0, -1):
        order += [k, chips - k]
    order.append(0)
    loads, shares = {}, {}
    for k in order:
        shares[k] = remote(
            part_ref.at[device(k, 1 - core)], paired.at[k], pair_send.at[k], pair_recv.at[k], partner
        )
        shares[k].start()
        loads[k] = pltpu.make_async_copy(part_ref.at[device(k, core)], mine.at[k], load_sem.at[k])
        loads[k].start()

    ready = set()

    def bring(k):
        if k not in ready:
            ready.add(k)
            loads[k].wait()
            shares[k].wait_recv()

    def index_of(dist, h):
        return 0 if dist == half_ring else 1 + 2 * (half_ring - 1 - dist) + h

    def await_ring(way, j):
        piece = arrived.at[way, j]
        remote(piece, piece, ring_send.at[way, j], ring_recv.at[way, j], ahead[way]).wait_recv()

    sends = []
    for dist in range(half_ring, 0, -1):
        for turn in (0, 1):
            for way in (0, 1):
                if dist == half_ring:
                    if turn == 1:
                        continue
                    h = way
                elif dist == half_ring - 1:
                    h = 1 - way if turn == 0 else way
                else:
                    h = turn
                k = dist if way == 0 else chips - dist
                bring(k)
                span = pl.ds(h * half, half)
                total = mine[k, span].astype(jnp.float32) + paired[k, span].astype(jnp.float32)
                has_prior = dist < half_ring - 1 or (dist == half_ring - 1 and h == way)
                if has_prior:
                    j = index_of(dist + 1, h)
                    await_ring(way, j)
                    total = total + arrived[way, j].astype(jnp.float32)
                mine[k, span] = total.astype(mine.dtype)
                j = index_of(dist, h)
                copy = remote(
                    mine.at[k, span], arrived.at[way, j],
                    ring_send.at[way, j], ring_recv.at[way, j], ahead[way],
                )
                copy.start()
                sends.append(copy)
    bring(0)
    for h in (0, 1):
        span = pl.ds(h * half, half)
        total = mine[0, span].astype(jnp.float32) + paired[0, span].astype(jnp.float32)
        for way in (0, 1):
            j = index_of(1, h)
            await_ring(way, j)
            total = total + arrived[way, j].astype(jnp.float32)
        out_ref[span] = total
    for copy in sends:
        copy.wait_send()
    for k in order:
        shares[k].wait_send()


def ring_reduce(part, n, collective_id):
    rows, cols = part.shape[1:]
    chips = n // 2
    return pl.pallas_call(
        functools.partial(reduce_kernel, n),
        out_shape=jax.ShapeDtypeStruct((rows, cols), jnp.float32),
        in_specs=[pl.BlockSpec(memory_space=pl.ANY)],
        out_specs=pl.BlockSpec(memory_space=pltpu.VMEM),
        scratch_shapes=[
            pltpu.VMEM((chips, rows, cols), part.dtype),
            pltpu.VMEM((chips, rows, cols), part.dtype),
            pltpu.VMEM((2, chips - 1, rows // 2, cols), part.dtype),
            pltpu.SemaphoreType.DMA((2, chips - 1)),
            pltpu.SemaphoreType.DMA((2, chips - 1)),
            pltpu.SemaphoreType.DMA((chips,)),
            pltpu.SemaphoreType.DMA((chips,)),
            pltpu.SemaphoreType.DMA((chips,)),
        ],
        compiler_params=pltpu.CompilerParams(
            collective_id=collective_id, has_side_effects=True, vmem_limit_bytes=60 * 1024 * 1024
        ),
        cost_estimate=pl.CostEstimate(flops=0, bytes_accessed=16 * part.size, transcendentals=0),
        name="ring_reduce_%d" % collective_id,
    )(part)


def shards(
    hidden,
    queries,
    latents,
    mem_latents,
    lengths,
    ids,
    gates,
    norm_gain,
    w_uv,
    w_out,
    w_gate,
    w_up,
    w_down,
):
    f32, bf16 = jnp.float32, jnp.bfloat16
    local_len, seq_count, model_width = hidden.shape[1:]
    latent_dim = latents.shape[3]
    head_count = queries.shape[3] // latent_dim
    row_count = local_len * seq_count
    n = lax.axis_size("expert")
    dp_size = lax.axis_size("dp")
    me = lax.axis_index("expert")
    core = me % 2
    own_dp = lax.axis_index("dp")
    heads_here, _, value_dim = w_uv.shape
    top_count = ids.shape[3]

    half_heads = heads_here // 2
    uv_half = lax.dynamic_slice_in_dim(w_uv, core * half_heads, half_heads, 0)
    out_half = lax.dynamic_slice_in_dim(
        w_out, core * half_heads * value_dim, half_heads * value_dim, 0
    )
    uv_groups, out_groups, starts = [w_uv], [w_out], [own_dp * heads_here]
    swap = [(i, i ^ 1) for i in range(n)]
    sizes = [heads_here]
    for shift in range(1, dp_size):
        turn = [(i, (i + shift) % dp_size) for i in range(dp_size)]
        source = (own_dp - shift + dp_size) % dp_size
        uv_far = lax.ppermute(uv_half, "dp", turn)
        out_far = lax.ppermute(out_half, "dp", turn)
        uv_near = lax.ppermute(uv_far, "expert", swap)
        out_near = lax.ppermute(out_far, "expert", swap)
        uv_groups += [uv_far, uv_near]
        out_groups += [out_far, out_near]
        starts += [
            source * heads_here + core * half_heads,
            source * heads_here + (1 - core) * half_heads,
        ]
        sizes += [half_heads, half_heads]

    latent_rows = jnp.transpose(latents[0], (1, 0, 2)).reshape(row_count, latent_dim)
    ids_t = jnp.transpose(ids[0], (2, 1, 0)).reshape(top_count, row_count).astype(bf16)
    gates_t = jnp.transpose(gates[0], (2, 1, 0)).reshape(top_count, row_count)
    table = jnp.concatenate([ids_t, gates_t], axis=0).reshape(-1)
    table_rows = -(-table.shape[0] // (16 * latent_dim)) * 16
    table = jnp.pad(table, (0, table_rows * latent_dim - table.shape[0]))
    packed = jnp.concatenate([latent_rows, table.reshape(table_rows, latent_dim)], axis=0)
    all_rows = row_count + table_rows
    cut = (all_rows // 2 + 15) // 16 * 16
    gathered = ring_gather(packed, n, cut, 0)

    segment = gathered[:, :row_count].reshape(n, seq_count, local_len, latent_dim)
    segment = jnp.transpose(segment, (1, 0, 2, 3)).reshape(seq_count, n * local_len, latent_dim)
    memory = jnp.transpose(mem_latents[0], (1, 0, 2))
    mem_count = memory.shape[1]
    keys = jnp.concatenate([memory, segment], axis=1)
    query_rows = jnp.transpose(
        queries[0].reshape(local_len, seq_count, head_count, latent_dim), (1, 2, 0, 3)
    ).reshape(seq_count, head_count * local_len, latent_dim)
    scores = jnp.einsum("sql,sjl->sqj", query_rows, keys, preferred_element_type=f32) * score_scale
    key_pos = jnp.arange(keys.shape[1], dtype=jnp.int32) - mem_count
    own_pos = me * local_len + jnp.arange(local_len, dtype=jnp.int32)
    visible = (key_pos[None, None, :] <= own_pos[None, :, None]) & (
        key_pos[None, None, :] < lengths[0][:, None, None]
    )
    visible = visible | (key_pos < 0)[None, None, :]
    scores = scores.reshape(seq_count, head_count, local_len, -1)
    scores = jnp.where(visible[:, None], scores, -jnp.inf)
    weights = jnp.exp(scores - jnp.max(scores, axis=3, keepdims=True))
    total = jnp.sum(weights, axis=3)
    attended = jnp.einsum(
        "sqj,sjl->sql",
        weights.astype(bf16).reshape(seq_count, head_count * local_len, -1),
        keys,
        preferred_element_type=f32,
    ).reshape(seq_count, head_count, local_len, latent_dim)
    attended = (attended / total[..., None]).astype(bf16)

    attn_out = jnp.zeros((row_count, model_width), f32)
    for uv, out, start, size in zip(uv_groups, out_groups, starts, sizes):
        heads = lax.dynamic_slice_in_dim(attended, start, size, 1)
        values = jnp.einsum("shtl,hlv->sthv", heads, uv, preferred_element_type=f32).astype(bf16)
        attn_out = attn_out + jnp.dot(
            values.reshape(row_count, size * value_dim), out, preferred_element_type=f32
        )

    hidden_rows = jnp.transpose(hidden[0], (1, 0, 2)).reshape(row_count, model_width)
    residual = hidden_rows.astype(f32) + attn_out
    mean_square = jnp.mean(residual * residual, axis=-1, keepdims=True)
    normed = (residual * lax.rsqrt(mean_square + norm_eps) * norm_gain.astype(f32)).astype(bf16)

    rows_all = ring_gather(normed, n, row_count // 2, 1)
    experts_here = w_gate.shape[0]
    expert_count = n * experts_here
    capacity = min(row_count, row_count * top_count // expert_count + 2)
    groups = n // 2
    wide = 2 * row_count
    slots = -(-2 * capacity // 16) * 16
    tables = gathered[:, row_count:].reshape(n, -1)[:, : 2 * top_count * row_count]
    tables = tables.reshape(groups, 2, 2, top_count, row_count)
    named = jnp.transpose(tables[:, :, 0], (2, 0, 1, 3)).reshape(top_count, groups, wide)
    scale = jnp.transpose(tables[:, :, 1], (2, 0, 1, 3)).reshape(top_count, groups, wide)
    rows_all = rows_all.reshape(groups, wide, model_width)
    steps = jnp.arange(wide, dtype=jnp.int32)
    earlier = (steps[:, None] < steps[None, :]).astype(bf16)
    partial = jnp.zeros((groups, wide, model_width), f32)
    for e in range(experts_here):
        matches = named == (me * experts_here + e).astype(bf16)
        hit = jnp.any(matches, axis=0)
        gate = jnp.sum(jnp.where(matches, scale.astype(f32), 0.0), axis=0)
        slot = jnp.dot(hit.astype(bf16), earlier, preferred_element_type=f32).astype(jnp.int32)
        slot = jnp.where(hit, slot, -1)
        chosen = slot[:, None, :] == jnp.arange(slots, dtype=jnp.int32)[None, :, None]
        placing = chosen.astype(bf16)
        mixing = jnp.where(chosen, gate[:, None, :], 0.0).astype(bf16)
        picked = jnp.einsum("gct,gtd->gcd", placing, rows_all, preferred_element_type=f32)
        picked = picked.astype(bf16).reshape(groups * slots, model_width)
        gate_h = jnp.dot(picked, w_gate[e], preferred_element_type=f32)
        up_h = jnp.dot(picked, w_up[e], preferred_element_type=f32)
        act = (jax.nn.silu(gate_h) * up_h).astype(bf16)
        produced = jnp.dot(act, w_down[e], preferred_element_type=f32).astype(bf16)
        partial = partial + jnp.einsum(
            "gct,gcd->gtd",
            mixing,
            produced.reshape(groups, slots, model_width),
            preferred_element_type=f32,
        )
    partial = partial.astype(bf16).reshape(n, row_count, model_width)
    routed = ring_reduce(partial, n, 2)
    layer_out = (residual + routed).astype(bf16).reshape(seq_count, local_len, model_width)
    return jnp.transpose(layer_out, (1, 0, 2))[None]


def solution(mesh):
    return jax.shard_map(
        shards,
        mesh=mesh,
        in_specs=(
            P("dp", "expert", None, None),
            P("dp", "expert", None, None),
            P("dp", "expert", None, None),
            P("dp", None, None, None),
            P("dp", None),
            P("dp", "expert", None, None),
            P("dp", "expert", None, None),
            P(),
            P("dp", None, None),
            P("dp", None),
            P("expert", None, None),
            P("expert", None, None),
            P("expert", None, None),
        ),
        out_specs=P("dp", "expert", None, None),
        check_vma=False,
    )
```

time: 318 us -> 194 us (0.61)
  the two profiles are of different devices: /device:TPU:13 before, /device:TPU:0 now
where the time goes in v1:
time: 194 us
  Pallas kernels  119 us (61%)
  matrix products  41 us (21%)
  local copies, waits for them, and re-layouts  22.1 us (11%)
  other arithmetic  8.16 us (4%)
  starting transfers between devices  3.55 us (2%)
    pallas_call x2, Pallas kernels, ring_gather(): pl.pallas_call(functools.partial(gather_kernel, n, cut), out_shape=jax.Sh...  70.3 us
    pallas_call x1, Pallas kernels, ring_reduce(): pl.pallas_call(functools.partial(reduce_kernel, n), out_shape=jax.ShapeDt...  48.3 us
    dot_general x1, matrix products, shards(): produced = jnp.dot(act, w_down[e], preferred_element_type=f32).astype(bf16)  11.6 us
    dot_general x1, matrix products, shards(): jnp.einsum('gct,gcd->gtd', mixing, produced.reshape(groups, slots, model_...  7.64 us
    dot_general x3, matrix products, shards(): jnp.dot(values.reshape(row_count, size * value_dim), out, preferred_eleme...  4.88 us
    dot_general x1, matrix products, shards(): up_h = jnp.dot(picked, w_up[e], preferred_element_type=f32)  4.8 us
    dot_general x1, matrix products, shards(): jnp.einsum('gct,gtd->gcd', placing, rows_all, preferred_element_type=f32)  4.77 us
  transfers between devices with their start and end apart: 4, of which 0 were waited for; matrix products, arithmetic and copies ran while one was open for 16% of the time, Pallas kernels for 12%

profile of v1, /device:TPU:0, one launch (start us, length us, event | category | flops | bytes accessed | tf_op | source)
XLA Modules:
  0.0 193.7 jit_solution(13450246746104416112)
XLA Ops:
  0.0 1.8 constant_dynamic-slice_fusion.1
  1.8 3.0 %collective-permute-start = (bf16[2,512,128]{2,1,0:T(8,128)(2,1)}, bf16[2,512,128]{2,1,0:T(8,128)(2,1)}, u32[]{:S(2)}, u32[]{:S(2)}) collective-permute-start(bf16[2,512,128]{2,1,0:T(8,128)(2,1)} %constant_dynamic-slice_fusion.1), channel_id=1, source_target_pairs={{0,16},{16,0},{1,17},{17,1},{2,18},{18,2},{3,19},{19,3},{4,20},{20... | collective-permute-start | bytes 786440 | tf_op jit(solution)/shard_map/ppermute | solution.py:290
  4.8 2.3 %constant_dynamic-slice_fusion = bf16[256,2048]{1,0:T(8,128)(2,1)} fusion(bf16[512,2048]{1,0:T(8,128)(2,1)} %param.22, s32[]{:T(128)S(6)} %select_n.52), kind=kLoop, calls=%fused_computation.75 | loop fusion | bytes 2097156 | tf_op jit(solution)/shard_map/dynamic_slice | solution.py:281
  7.1 0.8 reshape.175
  7.9 0.7 convert_bitcast_fusion.2
  8.6 0.1 convert_element_type.101
  8.7 0.9 copy.50
  9.7 0.7 pad_maximum_fusion.3.x_ref
  10.3 23.5 %ring_gather_0.1 = bf16[16,144,512]{2,1,0:T(8,128)(2,1)} custom-call(bf16[144,512]{1,0:T(8,128)(2,1)} %pad_maximum_fusion.3.x_ref), custom_call_target="tpu_custom_call" | custom-call | bytes 18874368 | tf_op jit(solution)/shard_map/ring_gather_0/pallas_call | solution.py:123
  33.9 0.6 copy-done.12
  34.6 0.1 broadcast_compare_fusion
  34.7 0.1 and_or_fusion
  34.8 0.3 broadcast_in_dim.53
  35.1 2.3 %copy.53 = pred[2,512,1056]{1,2,0:T(32,128)(4,1)} copy(pred[2,512,1056]{2,1,0:T(32,128)(4,1)S(1)} %bitcast.144) | data formatting | bytes 2162688 | tf_op jit(solution)/shard_map/jit(_where)/broadcast_in_dim | solution.py:329
  37.4 2.6 %reshape_squeeze.3 = bf16[64,2,8,512]{3,2,1,0:T(8,128)(2,1)} reshape(bf16[1,64,2,4096]{3,2,1,0:T(2,128)(2,1)} %param.14) | data formatting | bytes 2097152 | tf_op jit(solution)/shard_map/reshape;squeeze | solution.py:319
  40.0 2.0 %copy.52 = bf16[2,8,64,512]{3,2,1,0:T(8,128)(2,1)S(1)} copy(bf16[2,8,64,512]{3,1,0,2:T(8,128)(2,1)} %bitcast.146) | data formatting | bytes 2097152 | tf_op jit(solution)/shard_map/transpose | solution.py:318
  42.0 0.3 slice-done.1
  42.2 0.1 copy.51
  42.4 1.4 fusion.49
  43.8 2.9 %fusion.8 = f32[2,512,512]{2,1,0:T(8,128)} fusion(f32[2,512,1056]{1,2,0:T(8,128)S(1)} %get-tuple-element.6, f32[2,512]{1,0:T(2,128)S(1)} %get-tuple-element.5, bf16[2,1024,512]{2,1,0:T(8,128)(2,1)S(1)} %bitcast.151, bf16[2,32,512]{2,1,0:T(8,128)(2,1)S(1)} %bitcast.160), kind=kOutput, calls=%fused_computation.17 | convolution fusion | flops 1113784320 | bytes 8589312 | tf_op jit(solution)/shard_map/sqj,sjl->sql/dot_general | solution.py:332
  46.7 0.6 fusion
  47.3 0.4 slice-done
  47.7 0.1 copy.68
  47.8 0.1 reshape.186
  48.0 2.0 %fusion.11 = bf16[2,8,64,512]{3,2,0,1:T(8,128)(2,1)S(1)} fusion(f32[2,8,64,512]{3,2,1,0:T(8,128)} %bitcast.149, f32[2,8,64]{2,0,1:T(2,128)S(1)} %copy.54), kind=kLoop, calls=%fused_computation.21 | loop fusion | flops 1048576 | bytes 3149824 | tf_op jit(solution)/shard_map/convert_element_type | solution.py:338
  50.0 0.3 fusion.14
  50.3 0.1 copy.56
  50.4 1.4 fusion.30
  51.9 1.6 convert_bitcast_fusion
  53.5 0.5 collective-permute-start.3
  53.9 0.1 fusion.17
  54.1 0.1 collective-permute-start.2
  54.3 2.8 %copy.48 = f32[2,64,2048]{2,1,0:T(8,128)} copy(f32[2,64,2048]{2,0,1:T(2,128)} %convert_bitcast_fusion) | data formatting | bytes 2097152 | tf_op jit(solution)/shard_map/convert_element_type | solution.py:349
  57.1 1.3 fusion.15
  58.6 1.2 fusion.16
  59.8 1.9 convolution_add_fusion.1
  61.7 1.6 multiply_reduce_fusion
  63.4 1.0 copy-done.1
  64.4 0.9 multiply_convert_fusion.1.x_ref
  65.3 46.8 %ring_gather_1.1 = bf16[16,128,2048]{2,1,0:T(8,128)(2,1)} custom-call(bf16[128,2048]{1,0:T(8,128)(2,1)} %multiply_convert_fusion.1.x_ref), custom_call_target="tpu_custom_call" | custom-call | bytes 67108864 | tf_op jit(solution)/shard_map/ring_gather_1/pallas_call | solution.py:123
  112.1 4.8 %convolution_convert_fusion.2 = bf16[8,112,2048]{2,1,0:T(8,128)(2,1)S(1)} fusion(bf16[8,256,2048]{2,1,0:T(8,128)(2,1)} %bitcast.138, s32[8,256]{1,0:T(8,128)S(1)} %fusion.17), kind=kOutput, calls=%fused_computation.7 | convolution fusion | flops 941588480 | bytes 12066816 | tf_op jit(solution)/shard_map/gct,gtd->gcd/dot_general | solution.py:377
  116.9 1.8 copy-done.3
  118.7 4.8 %fusion.3 = f32[896,704]{0,1:T(8,128)} fusion(bf16[896,2048]{1,0:T(8,128)(2,1)S(1)} %bitcast.142, bf16[1,2048,704]{1,2,0:T(8,128)(2,1)S(1)} %copy-done.13), kind=kOutput, calls=%fused_computation.9 | convolution fusion | flops 2583691264 | bytes 9076736 | tf_op jit(solution)/shard_map/dot_general | solution.py:380
  123.5 11.6 %convolution_convert_fusion.1 = bf16[896,2048]{1,0:T(8,128)(2,1)} fusion(bf16[1,704,2048]{2,1,0:T(8,128)(2,1)S(1)} %copy-done, f32[896,704]{0,1:T(8,128)} %fusion.3, bf16[896,2048]{1,0:T(8,128)(2,1)} %bitcast.143, bf16[1,2048,704]{1,2,0:T(8,128)(2,1)} %param.23), kind=kOutput, calls=%fused_computation.6 | convolution fusion | flops 5173002240 | bytes 15630336 | tf_op jit(solution)/shard_map/dot_general | solution.py:382
  135.1 7.6 %convolution_convert_fusion = bf16[8,256,2048]{2,1,0:T(8,128)(2,1)} fusion(bf16[8,112,2048]{2,1,0:T(8,128)(2,1)} %bitcast.147, bf16[8,256]{1,0:T(8,128)(2,1)S(1)} %bitcast.161, s32[8,256]{1,0:T(8,128)S(1)} %fusion.17), kind=kOutput, calls=%fused_computation | convolution fusion | flops 944177152 | bytes 12070912 | tf_op jit(solution)/shard_map/gct,gcd->gtd/dot_general | solution.py:383
  142.8 48.3 %ring_reduce_2.1 = f32[128,2048]{1,0:T(8,128)} custom-call(bf16[16,128,2048]{2,1,0:T(8,128)(2,1)} %bitcast.139), custom_call_target="tpu_custom_call" | custom-call | bytes 67108864 | tf_op jit(solution)/shard_map/ring_reduce_2/pallas_call | solution.py:228
  191.1 1.3 add_convert_fusion
  192.4 1.3 copy.95
  (50 shorter events, 0.6 us)
Async XLA Ops:
  0.0 123.5 %copy-start = (bf16[1,704,2048]{2,1,0:T(8,128)(2,1)S(1)}, bf16[1,704,2048]{2,1,0:T(8,128)(2,1)}, u32[]{:S(2)}) copy-start(bf16[1,704,2048]{2,1,0:T(8,128)(2,1)} %param.25) | copy-start | bytes 8650756
  1.8 52.3 %collective-permute-start = (bf16[2,512,128]{2,1,0:T(8,128)(2,1)}, bf16[2,512,128]{2,1,0:T(8,128)(2,1)}, u32[]{:S(2)}, u32[]{:S(2)}) collective-permute-start(bf16[2,512,128]{2,1,0:T(8,128)(2,1)} %constant_dynamic-slice_fusion.1), channel_id=1, source_target_pairs={{0,16},{16,0},{1,17},{17,1},{2,18},{18,2},{3,19},{19,3},{4,20},{20... | collective-permute-start | bytes 786440 | tf_op jit(solution)/shard_map/ppermute | solution.py:290
  7.1 46.4 %collective-permute-start.1 = (bf16[256,2048]{1,0:T(8,128)(2,1)}, bf16[256,2048]{1,0:T(8,128)(2,1)}, u32[]{:S(2)}, u32[]{:S(2)}) collective-permute-start(bf16[256,2048]{1,0:T(8,128)(2,1)} %constant_dynamic-slice_fusion), channel_id=1, source_target_pairs={{0,16},{16,0},{1,17},{17,1},{2,18},{18,2},{3,19},{19,3},{4,20},{20... | collective-permute-start | bytes 3145736 | tf_op jit(solution)/shard_map/ppermute | solution.py:291
  33.8 0.7 copy-start.12
  33.9 0.8 copy-start.10
  40.0 2.2 %slice-start.1 = ((bf16[16,144,512]{2,1,0:T(8,128)(2,1)}), bf16[16,128,512]{2,1,0:T(8,128)(2,1)S(1)}, s32[]{:S(2)}) async-start(bf16[16,144,512]{2,1,0:T(8,128)(2,1)} %ring_gather_0.1), calls=%async_computation.1 | async-start | bytes 4194304 | tf_op jit(solution)/shard_map/slice | solution.py:313
  40.0 2.4 %copy-start.8 = (pred[2,512,1056]{1,2,0:T(32,128)(4,1)S(1)}, pred[2,512,1056]{1,2,0:T(32,128)(4,1)}, u32[]{:S(2)}) copy-start(pred[2,512,1056]{1,2,0:T(32,128)(4,1)} %copy.53) | copy-start | bytes 3244036
  46.7 0.9 slice-start
  47.8 2.2 %copy-start.7 = (bf16[4,512,128]{2,1,0:T(8,128)(2,1)S(1)}, bf16[4,512,128]{2,1,0:T(8,128)(2,1)}, u32[]{:S(2)}) copy-start(bf16[4,512,128]{2,1,0:T(8,128)(2,1)} %param.21) | copy-start | bytes 1572868
  48.0 2.4 %copy-start.4 = (bf16[512,2048]{1,0:T(8,128)(2,1)S(1)}, bf16[512,2048]{1,0:T(8,128)(2,1)}, u32[]{:S(2)}) copy-start(bf16[512,2048]{1,0:T(8,128)(2,1)} %param.22) | copy-start | bytes 6291460
  50.0 3.4 %copy-start.6 = (bf16[2,8,64,512]{3,2,0,1:T(8,128)(2,1)}, bf16[2,8,64,512]{3,2,0,1:T(8,128)(2,1)S(1)}, u32[]{:S(2)}) copy-start(bf16[2,8,64,512]{3,2,0,1:T(8,128)(2,1)S(1)} %fusion.11) | copy-start | bytes 3145732
  50.0 1.9 copy-start.9
  50.3 4.0 %copy-start.11 = (bf16[2048]{0:T(1024)(128)(2,1)S(1)}, bf16[2048]{0:T(1024)(128)(2,1)}, u32[]{:S(2)}) copy-start(bf16[2048]{0:T(1024)(128)(2,1)} %param.20) | copy-start | bytes 12292
  53.5 8.2 %collective-permute-start.3 = (bf16[256,2048]{1,0:T(8,128)(2,1)}, bf16[256,2048]{1,0:T(8,128)(2,1)}, u32[]{:S(2)}, u32[]{:S(2)}) collective-permute-start(bf16[256,2048]{1,0:T(8,128)(2,1)} %collective-permute-done.1), channel_id=1, source_target_pairs={{0,1},{1,0},{2,3},{3,2},{4,5},{5,4},{6,7},{7,6},{8,9},{9,8},{10,11... | collective-permute-start | bytes 3145736 | tf_op jit(solution)/shard_map/ppermute | solution.py:293
  54.1 4.5 %collective-permute-start.2 = (bf16[2,512,128]{2,1,0:T(8,128)(2,1)}, bf16[2,512,128]{2,1,0:T(8,128)(2,1)S(1)}, u32[]{:S(2)}, u32[]{:S(2)}) collective-permute-start(bf16[2,512,128]{2,1,0:T(8,128)(2,1)} %collective-permute-done), channel_id=1, source_target_pairs={{0,1},{1,0},{2,3},{3,2},{4,5},{5,4},{6,7},{7,6},{8,9},{9,8},{10,11... | collective-permute-start | bytes 786440 | tf_op jit(solution)/shard_map/ppermute | solution.py:292
  57.1 4.6 %copy-start.5 = (f32[2,64,2048]{2,1,0:T(8,128)S(1)}, f32[2,64,2048]{2,1,0:T(8,128)}, u32[]{:S(2)}) copy-start(f32[2,64,2048]{2,1,0:T(8,128)} %copy.48) | copy-start | bytes 3145732
  63.3 1.0 copy-start.1
  112.1 6.6 %copy-start.13 = (bf16[1,2048,704]{1,2,0:T(8,128)(2,1)S(1)}, bf16[1,2048,704]{1,2,0:T(8,128)(2,1)}, u32[]{:S(2)}) copy-start(bf16[1,2048,704]{1,2,0:T(8,128)(2,1)} %param.24) | copy-start | bytes 8650756
  116.9 1.8 copy-start.3
  142.8 48.3 %copy-start.2 = (f32[128,2048]{1,0:T(8,128)S(1)}, f32[128,2048]{1,0:T(8,128)}, u32[]{:S(2)}) copy-start(f32[128,2048]{1,0:T(8,128)} %copy-done.1) | copy-start | bytes 3145732

commit v2 on v1

--- a/solution.py
+++ b/solution.py
@@ -139,7 +139,7 @@
 
 
 def reduce_kernel(
-    n, part_ref, out_ref, mine, paired, arrived, ring_send, ring_recv, pair_send, pair_recv, load_sem
+    n, rows_ref, mix_ref, out_ref, mine, paired, give, arrived, ring_send, ring_recv, pair_send, pair_recv
 ):
     chips = n // 2
     half_ring = chips // 2
@@ -154,21 +154,31 @@
     for k in range(half_ring - 1, 0, -1):
         order += [k, chips - k]
     order.append(0)
-    loads, shares = {}, {}
-    for k in order:
-        shares[k] = remote(
-            part_ref.at[device(k, 1 - core)], paired.at[k], pair_send.at[k], pair_recv.at[k], partner
-        )
+    depth = give.shape[0]
+    shares, made, seen = {}, [], set()
+
+    def weigh(k, core_of):
+        dest = device(k, core_of)
+        return jnp.dot(
+            mix_ref[dest], rows_ref[dest // 2], preferred_element_type=jnp.float32
+        ).astype(mine.dtype)
+
+    def make():
+        k = order[len(made)]
+        slot = len(made) % depth
+        if len(made) >= depth:
+            shares[order[len(made) - depth]].wait_send()
+        give[slot] = weigh(k, 1 - core)
+        shares[k] = remote(give.at[slot], paired.at[k], pair_send.at[k], pair_recv.at[k], partner)
         shares[k].start()
-        loads[k] = pltpu.make_async_copy(part_ref.at[device(k, core)], mine.at[k], load_sem.at[k])
-        loads[k].start()
-
-    ready = set()
+        mine[k] = weigh(k, core)
+        made.append(k)
 
     def bring(k):
-        if k not in ready:
-            ready.add(k)
-            loads[k].wait()
+        while k not in made or (len(made) < chips and len(made) < order.index(k) + 3):
+            make()
+        if k not in seen:
+            seen.add(k)
             shares[k].wait_recv()
 
     def index_of(dist, h):
@@ -218,34 +228,38 @@
         out_ref[span] = total
     for copy in sends:
         copy.wait_send()
-    for k in order:
+    for k in order[chips - min(depth, chips) :]:
         shares[k].wait_send()
 
 
-def ring_reduce(part, n, collective_id):
-    rows, cols = part.shape[1:]
+def ring_reduce(rows_in, mix, n, collective_id):
+    rows = mix.shape[1]
+    cols = rows_in.shape[2]
     chips = n // 2
+    dtype = rows_in.dtype
     return pl.pallas_call(
         functools.partial(reduce_kernel, n),
         out_shape=jax.ShapeDtypeStruct((rows, cols), jnp.float32),
-        in_specs=[pl.BlockSpec(memory_space=pl.ANY)],
+        in_specs=[pl.BlockSpec(memory_space=pltpu.VMEM)] * 2,
         out_specs=pl.BlockSpec(memory_space=pltpu.VMEM),
         scratch_shapes=[
-            pltpu.VMEM((chips, rows, cols), part.dtype),
-            pltpu.VMEM((chips, rows, cols), part.dtype),
-            pltpu.VMEM((2, chips - 1, rows // 2, cols), part.dtype),
+            pltpu.VMEM((chips, rows, cols), dtype),
+            pltpu.VMEM((chips, rows, cols), dtype),
+            pltpu.VMEM((min(4, chips), rows, cols), dtype),
+            pltpu.VMEM((2, chips - 1, rows // 2, cols), dtype),
             pltpu.SemaphoreType.DMA((2, chips - 1)),
             pltpu.SemaphoreType.DMA((2, chips - 1)),
             pltpu.SemaphoreType.DMA((chips,)),
             pltpu.SemaphoreType.DMA((chips,)),
-            pltpu.SemaphoreType.DMA((chips,)),
         ],
         compiler_params=pltpu.CompilerParams(
-            collective_id=collective_id, has_side_effects=True, vmem_limit_bytes=60 * 1024 * 1024
+            collective_id=collective_id, has_side_effects=True, vmem_limit_bytes=62 * 1024 * 1024
         ),
-        cost_estimate=pl.CostEstimate(flops=0, bytes_accessed=16 * part.size, transcendentals=0),
+        cost_estimate=pl.CostEstimate(
+            flops=2 * mix.size * cols, bytes_accessed=16 * n * rows * cols, transcendentals=0
+        ),
         name="ring_reduce_%d" % collective_id,
-    )(part)
+    )(rows_in, mix)
 
 
 def shards(
@@ -319,23 +333,15 @@
         queries[0].reshape(local_len, seq_count, head_count, latent_dim), (1, 2, 0, 3)
     ).reshape(seq_count, head_count * local_len, latent_dim)
     scores = jnp.einsum("sql,sjl->sqj", query_rows, keys, preferred_element_type=f32) * score_scale
-    key_pos = jnp.arange(keys.shape[1], dtype=jnp.int32) - mem_count
-    own_pos = me * local_len + jnp.arange(local_len, dtype=jnp.int32)
-    visible = (key_pos[None, None, :] <= own_pos[None, :, None]) & (
-        key_pos[None, None, :] < lengths[0][:, None, None]
-    )
-    visible = visible | (key_pos < 0)[None, None, :]
-    scores = scores.reshape(seq_count, head_count, local_len, -1)
-    scores = jnp.where(visible[:, None], scores, -jnp.inf)
-    weights = jnp.exp(scores - jnp.max(scores, axis=3, keepdims=True))
-    total = jnp.sum(weights, axis=3)
-    attended = jnp.einsum(
-        "sqj,sjl->sql",
-        weights.astype(bf16).reshape(seq_count, head_count * local_len, -1),
-        keys,
-        preferred_element_type=f32,
-    ).reshape(seq_count, head_count, local_len, latent_dim)
-    attended = (attended / total[..., None]).astype(bf16)
+    key_pos = lax.broadcasted_iota(jnp.int32, scores.shape, 2) - mem_count
+    own_pos = me * local_len + lax.broadcasted_iota(jnp.int32, scores.shape, 1) % local_len
+    visible = (key_pos <= own_pos) & (key_pos < lengths[0][:, None, None])
+    scores = jnp.where(visible | (key_pos < 0), scores, -jnp.inf)
+    weights = jnp.exp(scores - jnp.max(scores, axis=2, keepdims=True))
+    total = jnp.sum(weights, axis=2, keepdims=True)
+    attended = jnp.einsum("sqj,sjl->sql", weights.astype(bf16), keys, preferred_element_type=f32)
+    attended = (attended / total).astype(bf16)
+    attended = attended.reshape(seq_count, head_count, local_len, latent_dim)
 
     attn_out = jnp.zeros((row_count, model_width), f32)
     for uv, out, start, size in zip(uv_groups, out_groups, starts, sizes):
@@ -346,7 +352,7 @@
         )
 
     hidden_rows = jnp.transpose(hidden[0], (1, 0, 2)).reshape(row_count, model_width)
-    residual = hidden_rows.astype(f32) + attn_out
+    residual = lax.optimization_barrier(hidden_rows).astype(f32) + attn_out
     mean_square = jnp.mean(residual * residual, axis=-1, keepdims=True)
     normed = (residual * lax.rsqrt(mean_square + norm_eps) * norm_gain.astype(f32)).astype(bf16)
 
@@ -364,7 +370,7 @@
     rows_all = rows_all.reshape(groups, wide, model_width)
     steps = jnp.arange(wide, dtype=jnp.int32)
     earlier = (steps[:, None] < steps[None, :]).astype(bf16)
-    partial = jnp.zeros((groups, wide, model_width), f32)
+    made_rows, mixes = [], []
     for e in range(experts_here):
         matches = named == (me * experts_here + e).astype(bf16)
         hit = jnp.any(matches, axis=0)
@@ -373,21 +379,19 @@
         slot = jnp.where(hit, slot, -1)
         chosen = slot[:, None, :] == jnp.arange(slots, dtype=jnp.int32)[None, :, None]
         placing = chosen.astype(bf16)
-        mixing = jnp.where(chosen, gate[:, None, :], 0.0).astype(bf16)
+        slot_t = jnp.where(hit, slot, -1).reshape(n, row_count)
+        chosen_t = slot_t[:, :, None] == jnp.arange(slots, dtype=jnp.int32)[None, None, :]
+        mixes.append(jnp.where(chosen_t, gate.reshape(n, row_count)[:, :, None], 0.0).astype(bf16))
         picked = jnp.einsum("gct,gtd->gcd", placing, rows_all, preferred_element_type=f32)
         picked = picked.astype(bf16).reshape(groups * slots, model_width)
         gate_h = jnp.dot(picked, w_gate[e], preferred_element_type=f32)
         up_h = jnp.dot(picked, w_up[e], preferred_element_type=f32)
         act = (jax.nn.silu(gate_h) * up_h).astype(bf16)
         produced = jnp.dot(act, w_down[e], preferred_element_type=f32).astype(bf16)
-        partial = partial + jnp.einsum(
-            "gct,gcd->gtd",
-            mixing,
-            produced.reshape(groups, slots, model_width),
-            preferred_element_type=f32,
-        )
-    partial = partial.astype(bf16).reshape(n, row_count, model_width)
-    routed = ring_reduce(partial, n, 2)
+        made_rows.append(produced.reshape(groups, slots, model_width))
+    made_rows = made_rows[0] if experts_here == 1 else jnp.concatenate(made_rows, axis=1)
+    mixing = mixes[0] if experts_here == 1 else jnp.concatenate(mixes, axis=2)
+    routed = ring_reduce(made_rows, mixing, n, 2)
     layer_out = (residual + routed).astype(bf16).reshape(seq_count, local_len, model_width)
     return jnp.transpose(layer_out, (1, 0, 2))[None]
 

time: 194 us -> 181 us (0.933)
  matrix products: 41 us -> 31.9 us
  local copies, waits for them, and re-layouts: 22.1 us -> 17.9 us
  other arithmetic: 8.16 us -> 5.07 us
  Pallas kernels: 119 us -> 121 us
    dot_general x2 -> x1, matrix products: 10.5 us -> 1.7 us  [shards(): jnp.einsum('sqj,sjl->sql', weights.astype(bf16), keys, preferred_element_...]
    convert_element_type x1 -> x0, local copies, waits for them, and re-layouts: 2.83 us -> none  [shards(): residual = hidden_rows.astype(f32) + attn_out]
    pallas_call x1, Pallas kernels: 48.3 us -> 51 us  [ring_reduce(): pl.pallas_call(functools.partial(reduce_kernel, n), out_shape=jax.ShapeDt...]
    broadcast_in_dim x2 -> x0, local copies, waits for them, and re-layouts: 2.6 us -> none  [shards(): scores = jnp.where(visible[:, None], scores, -jnp.inf)]
    dot_general x1, matrix products: 1.43 us -> 3.72 us  [shards(): jnp.einsum('sql,sjl->sqj', query_rows, keys, preferred_element_type=f32)]
    convert_element_type x2 -> x1, other arithmetic: 3.52 us -> 1.37 us  [shards(): jnp.where(chosen_t, gate.reshape(n, row_count)[:, :, None], 0.0)]
    dot_general x3, matrix products: 4.88 us -> 2.79 us  [shards(): jnp.dot(values.reshape(row_count, size * value_dim), out, preferred_eleme...]
    unnamed x31 -> x22, local copies, waits for them, and re-layouts: 3.64 us -> 5 us
  transfers between devices with their start and end apart: 4 -> 4, of which waited for: 0 -> 0; matrix products, arithmetic and copies ran while one was open for 16% -> 12% of each run, Pallas kernels for 12% -> 13%
where the time goes in v2:
time: 181 us; the launch traced here: 180 us
  Pallas kernels  121 us (67%)
  matrix products  31.9 us (18%)
  local copies, waits for them, and re-layouts  17.9 us (10%)
  other arithmetic  5.07 us (3%)
  starting transfers between devices  3.64 us (2%)
    pallas_call x2, Pallas kernels, ring_gather(): pl.pallas_call(functools.partial(gather_kernel, n, cut), out_shape=jax.Sh...  70.5 us
    pallas_call x1, Pallas kernels, ring_reduce(): pl.pallas_call(functools.partial(reduce_kernel, n), out_shape=jax.ShapeDt...  51 us
    dot_general x1, matrix products, shards(): produced = jnp.dot(act, w_down[e], preferred_element_type=f32).astype(bf16)  12.4 us
    unnamed x22, local copies, waits for them, and re-layouts  5 us
    dot_general x1, matrix products, shards(): jnp.einsum('gct,gtd->gcd', placing, rows_all, preferred_element_type=f32)  4.79 us
    dot_general x1, matrix products, shards(): up_h = jnp.dot(picked, w_up[e], preferred_element_type=f32)  4.72 us
    dot_general x1, matrix products, shards(): jnp.einsum('sql,sjl->sqj', query_rows, keys, preferred_element_type=f32)  3.72 us
  transfers between devices with their start and end apart: 4, of which 0 were waited for; matrix products, arithmetic and copies ran while one was open for 12% of the time, Pallas kernels for 13%

profile of v2, /device:TPU:0, one launch (start us, length us, event | category | flops | bytes accessed | tf_op | source)
XLA Modules:
  0.0 180.4 jit_solution(15198277275547799506)
XLA Ops:
  0.0 1.0 copy-done
  1.1 3.0 %collective-permute-start = (bf16[2,512,128]{2,1,0:T(8,128)(2,1)S(1)}, bf16[2,512,128]{2,1,0:T(8,128)(2,1)}, u32[]{:S(2)}, u32[]{:S(2)}) collective-permute-start(bf16[2,512,128]{2,1,0:T(8,128)(2,1)S(1)} %constant_dynamic-slice_fusion.3), channel_id=1, source_target_pairs={{0,16},{16,0},{1,17},{17,1},{2,18},{18,2},{3,19},{19,3},{4,20},{20... | collective-permute-start | bytes 786440 | tf_op jit(solution)/shard_map/ppermute | solution.py:304
  4.1 2.3 %constant_dynamic-slice_fusion.1 = bf16[256,2048]{1,0:T(8,128)(2,1)} fusion(bf16[512,2048]{1,0:T(8,128)(2,1)} %param.22, s32[]{:T(128)S(6)} %select_n.59), kind=kLoop, calls=%fused_computation.75 | loop fusion | bytes 2097156 | tf_op jit(solution)/shard_map/dynamic_slice | solution.py:295
  6.4 0.0 collective-permute-start.1
  6.5 0.9 copy.52
  7.4 0.1 convert_element_type.85
  7.5 0.1 reshape.83
  7.7 0.7 pad_maximum_fusion.5.x_ref
  8.3 23.6 %ring_gather_0.1 = bf16[16,144,512]{2,1,0:T(8,128)(2,1)} custom-call(bf16[144,512]{1,0:T(8,128)(2,1)} %pad_maximum_fusion.5.x_ref), custom_call_target="tpu_custom_call" | custom-call | bytes 18874368 | tf_op jit(solution)/shard_map/ring_gather_0/pallas_call | solution.py:123
  32.0 0.0 slice-start
  32.0 0.0 copy-start.4
  32.0 1.6 slice-done
  33.6 1.5 copy.53
  35.1 1.8 reshape_squeeze.3
  36.9 0.6 copy.54
  37.5 3.7 %fusion.49 = (f32[2,512]{1,0:T(2,128)S(1)}, f32[2,512,1056]{1,2,0:T(8,128)S(1)}) fusion(bf16[2,512,512]{2,1,0:T(8,128)(2,1)S(1)} %bitcast.144, bf16[2,1024,512]{2,1,0:T(8,128)(2,1)} %bitcast.141, bf16[2,32,512]{2,1,0:T(8,128)(2,1)S(1)} %bitcast.154, pred[1056]{0:T(1024)(128)(4,1)S(1)} %broadcast_compare_fusion, s32[2]{0:T(128)S(1)} %bitcast.159, ...), kind=kOutput, calls=%fused_computation.83 | convolution fusion | flops 1121352704 | bytes 7550636 | tf_op jit(solution)/shard_map/sql,sjl->sqj/dot_general | solution.py:335
  41.3 0.6 fusion.2
  41.9 1.0 copy-done.2
  42.9 1.7 divide_convert_fusion
  44.6 1.0 copy-done.3
  45.6 0.3 fusion.15
  45.9 0.1 copy.56
  46.0 0.2 copy.73
  46.1 0.1 reshape.94
  46.3 0.2 bitcast_select_fusion.1
  46.4 2.1 %fusion.30 = f32[128,2048]{1,0:T(8,128)S(1)} fusion(bf16[512,2048]{1,0:T(8,128)(2,1)} %param.22, bf16[16,8,4,128]{3,2,1,0:T(4,128)(2,1)S(1)} %bitcast.145), kind=kOutput, calls=%fused_computation.47 | convolution fusion | flops 268435456 | bytes 3276800 | tf_op jit(solution)/shard_map/dot_general | solution.py:350
  48.6 0.0 collective-permute-done.1
  48.6 0.5 collective-permute-start.3
  49.0 1.4 select_convert_fusion.mix_ref
  50.4 0.1 collective-permute-start.2
  50.5 1.1 constant_dynamic-slice_fusion
  51.6 1.2 copy.50
  52.8 1.2 fusion.16
  54.0 0.1 copy.58
  54.1 0.2 fusion.17
  54.3 0.1 copy.60
  54.4 0.3 convolution_add_fusion.1
  54.7 0.4 multiply_reduce_fusion
  55.2 1.0 multiply_convert_fusion.1.x_ref
  56.1 46.9 %ring_gather_1.1 = bf16[16,128,2048]{2,1,0:T(8,128)(2,1)} custom-call(bf16[128,2048]{1,0:T(8,128)(2,1)} %multiply_convert_fusion.1.x_ref), custom_call_target="tpu_custom_call" | custom-call | bytes 67108864 | tf_op jit(solution)/shard_map/ring_gather_1/pallas_call | solution.py:123
  103.0 0.0 copy-start.8
  103.0 4.8 %convolution_convert_fusion.1 = bf16[8,112,2048]{2,1,0:T(8,128)(2,1)S(1)} fusion(bf16[8,256,2048]{2,1,0:T(8,128)(2,1)} %bitcast.133, s32[8,256]{1,0:T(8,128)S(1)} %get-tuple-element.12), kind=kOutput, calls=%fused_computation.9 | convolution fusion | flops 941588480 | bytes 12066816 | tf_op jit(solution)/shard_map/gct,gtd->gcd/dot_general | solution.py:385
  107.8 1.8 %copy-done.1 = bf16[8,112,2048]{2,1,0:T(8,128)(2,1)} copy-done((bf16[8,112,2048]{2,1,0:T(8,128)(2,1)}, bf16[8,112,2048]{2,1,0:T(8,128)(2,1)S(1)}, u32[]{:S(2)}) %copy-start.1) | copy-done | bytes 3670040
  109.6 4.7 %fusion.5 = f32[896,704]{0,1:T(8,128)} fusion(bf16[896,2048]{1,0:T(8,128)(2,1)S(1)} %bitcast.136, bf16[1,2048,704]{1,2,0:T(8,128)(2,1)S(1)} %copy-done.8), kind=kOutput, calls=%fused_computation.11 | convolution fusion | flops 2583691264 | bytes 9076736 | tf_op jit(solution)/shard_map/dot_general | solution.py:388
  114.4 12.4 %convolution_convert_fusion = bf16[896,2048]{1,0:T(8,128)(2,1)} fusion(bf16[1,704,2048]{2,1,0:T(8,128)(2,1)} %param.25, f32[896,704]{0,1:T(8,128)} %fusion.5, bf16[896,2048]{1,0:T(8,128)(2,1)} %bitcast.137, bf16[1,2048,704]{1,2,0:T(8,128)(2,1)} %param.23), kind=kOutput, calls=%fused_computation.8 | convolution fusion | flops 5173002240 | bytes 15630336 | tf_op jit(solution)/shard_map/dot_general | solution.py:390
  126.7 51.0 %ring_reduce_2.1 = f32[128,2048]{1,0:T(8,128)} custom-call(bf16[8,112,2048]{2,1,0:T(8,128)(2,1)} %bitcast.139, bf16[16,128,112]{2,1,0:T(8,128)(2,1)} %select_convert_fusion.mix_ref), custom_call_target="tpu_custom_call" | custom-call | flops 939524096 | bytes 67108864 | tf_op jit(solution)/shard_map/ring_reduce_2/pallas_call | solution.py:240
  177.7 1.3 add_convert_fusion
  179.1 1.3 copy.104
  (35 shorter events, 0.2 us)
Async XLA Ops:
  0.0 1.0 copy-start
  0.0 7.4 %copy-start.5 = (s32[1,64,2,6]{1,2,3,0:T(2,128)S(1)}, s32[1,64,2,6]{1,2,3,0:T(2,128)}, u32[]{:S(2)}) copy-start(s32[1,64,2,6]{1,2,3,0:T(2,128)} %param.18) | copy-start | bytes 9220
  0.0 7.5 %copy-start.7 = (bf16[1,64,2,6]{1,2,3,0:T(2,128)(2,1)S(1)}, bf16[1,64,2,6]{1,2,3,0:T(2,128)(2,1)}, u32[]{:S(2)}) copy-start(bf16[1,64,2,6]{1,2,3,0:T(2,128)(2,1)} %param.19) | copy-start | bytes 4612
  1.1 49.4 %collective-permute-start = (bf16[2,512,128]{2,1,0:T(8,128)(2,1)S(1)}, bf16[2,512,128]{2,1,0:T(8,128)(2,1)}, u32[]{:S(2)}, u32[]{:S(2)}) collective-permute-start(bf16[2,512,128]{2,1,0:T(8,128)(2,1)S(1)} %constant_dynamic-slice_fusion.3), channel_id=1, source_target_pairs={{0,16},{16,0},{1,17},{17,1},{2,18},{18,2},{3,19},{19,3},{4,20},{20... | collective-permute-start | bytes 786440 | tf_op jit(solution)/shard_map/ppermute | solution.py:304
  6.4 42.1 %collective-permute-start.1 = (bf16[256,2048]{1,0:T(8,128)(2,1)}, bf16[256,2048]{1,0:T(8,128)(2,1)S(1)}, u32[]{:S(2)}, u32[]{:S(2)}) collective-permute-start(bf16[256,2048]{1,0:T(8,128)(2,1)} %constant_dynamic-slice_fusion.1), channel_id=1, source_target_pairs={{0,16},{16,0},{1,17},{17,1},{2,18},{18,2},{3,19},{19,3},{4,20},{20... | collective-permute-start | bytes 3145736 | tf_op jit(solution)/shard_map/ppermute | solution.py:305
  32.0 1.6 slice-start
  32.0 3.1 %copy-start.4 = (bf16[1,32,2,512]{3,2,1,0:T(2,128)(2,1)S(1)}, bf16[1,32,2,512]{3,2,1,0:T(2,128)(2,1)}, u32[]{:S(2)}) copy-start(bf16[1,32,2,512]{3,2,1,0:T(2,128)(2,1)} %param.16) | copy-start | bytes 196612
  35.1 2.4 %copy-start.9 = (s32[1,2]{1,0:T(1,128)S(1)}, s32[1,2]{1,0:T(1,128)}, u32[]{:S(2)}) copy-start(s32[1,2]{1,0:T(1,128)} %param.17) | copy-start | bytes 28
  41.3 1.6 copy-start.2
  42.9 3.1 %slice-start.1 = ((bf16[16,144,512]{2,1,0:T(8,128)(2,1)}), bf16[16,16,512]{2,1,0:T(8,128)(2,1)S(1)}, s32[]{:S(2)}) async-start(bf16[16,144,512]{2,1,0:T(8,128)(2,1)} %ring_gather_0.1), calls=%async_computation.1 | async-start | bytes 524288 | tf_op jit(solution)/shard_map/slice | solution.py:366
  44.6 1.0 copy-start.3
  46.4 6.4 %copy-start.6 = (bf16[2048]{0:T(1024)(128)(2,1)S(1)}, bf16[2048]{0:T(1024)(128)(2,1)}, u32[]{:S(2)}) copy-start(bf16[2048]{0:T(1024)(128)(2,1)} %param.20) | copy-start | bytes 12292
  48.6 6.1 %collective-permute-start.3 = (bf16[256,2048]{1,0:T(8,128)(2,1)S(1)}, bf16[256,2048]{1,0:T(8,128)(2,1)S(1)}, u32[]{:S(2)}, u32[]{:S(2)}) collective-permute-start(bf16[256,2048]{1,0:T(8,128)(2,1)S(1)} %collective-permute-done.1), channel_id=1, source_target_pairs={{0,1},{1,0},{2,3},{3,2},{4,5},{5,4},{6,7},{7,6},{8,9},{9,8},{10,11... | collective-permute-start | bytes 3145736 | tf_op jit(solution)/shard_map/ppermute | solution.py:307
  50.4 3.7 %collective-permute-start.2 = (bf16[2,512,128]{2,1,0:T(8,128)(2,1)}, bf16[2,512,128]{2,1,0:T(8,128)(2,1)S(1)}, u32[]{:S(2)}, u32[]{:S(2)}) collective-permute-start(bf16[2,512,128]{2,1,0:T(8,128)(2,1)} %collective-permute-done), channel_id=1, source_target_pairs={{0,1},{1,0},{2,3},{3,2},{4,5},{5,4},{6,7},{7,6},{8,9},{9,8},{10,11... | collective-permute-start | bytes 786440 | tf_op jit(solution)/shard_map/ppermute | solution.py:306
  103.0 6.6 %copy-start.8 = (bf16[1,2048,704]{1,2,0:T(8,128)(2,1)S(1)}, bf16[1,2048,704]{1,2,0:T(8,128)(2,1)}, u32[]{:S(2)}) copy-start(bf16[1,2048,704]{1,2,0:T(8,128)(2,1)} %param.24) | copy-start | bytes 8650756
  107.8 1.8 %copy-start.1 = (bf16[8,112,2048]{2,1,0:T(8,128)(2,1)}, bf16[8,112,2048]{2,1,0:T(8,128)(2,1)S(1)}, u32[]{:S(2)}) copy-start(bf16[8,112,2048]{2,1,0:T(8,128)(2,1)S(1)} %convolution_convert_fusion.1) | copy-start | bytes 11010052
